TPU v7x, 8 devices: a whole 2x2x1 slice. The times are simulated.
8 devices in a mesh: dp: 1 (over z), col: 2 (over y), row: 4 (over x, core).
Axes of the slice: x: 2, y: 2, z: 1, core: 2. Of those that a mesh axis runs over, the one named last changes fastest.
Arguments:
- seq_in: bfloat16 [128, 32, 2560], P(None, 'dp', 'row')
- w_in1: bfloat16 [2560, 10240], P('row', 'col')
- w_rec1: bfloat16 [2560, 10240], P('row', 'col')
- b_gate1: float32 [10240], P(('col', 'row'))
- w_in2: bfloat16 [2560, 10240], P('row', 'col')
- w_rec2: bfloat16 [2560, 10240], P('row', 'col')
- b_gate2: float32 [10240], P(('col', 'row'))
- h_init: float32 [2, 32, 2560], P(None, 'dp', 'row')
- c_init: float32 [2, 32, 2560], P(None, 'dp', 'row')
Outputs:
- output 1: bfloat16 [128, 32, 2560], P(None, 'dp', ('row', 'col'))
- output 2: float32 [32, 2560], P('dp', ('row', 'col'))
- output 3: float32 [32, 2560], P('dp', ('row', 'col'))
All inputs are finite; a program needn't handle non-finite values.
Results may differ from a plain program's by a relative error of at most 0.00360462.
Values are sent between devices in bfloat16 or wider.
A program may use at most 1 GiB of HBM per device.

v0:
```python
import jax
import jax.numpy as jnp
from jax import lax
from jax.sharding import PartitionSpec as P


def gate_update(z_own, c_prev):
    unit_dev = c_prev.shape[-1]
    in_gate = jax.nn.sigmoid(z_own[:, :unit_dev])
    forget = jax.nn.sigmoid(z_own[:, unit_dev:2 * unit_dev])
    cell_in = jnp.tanh(z_own[:, 2 * unit_dev:3 * unit_dev])
    out_gate = jax.nn.sigmoid(z_own[:, 3 * unit_dev:])
    c_new = forget * c_prev + in_gate * cell_in
    h_new = (out_gate * jnp.tanh(c_new)).astype(jnp.bfloat16)
    return h_new, c_new


def solution(mesh):
    def lstm_layer(in_rows, w_in, w_rec, b_own, h_rows, c_own, keep_rows):
        def lstm_step(carry_in, in_step):
            h_prev, c_prev = carry_in
            part_sum = jnp.dot(in_step, w_in, preferred_element_type=jnp.float32)
            part_sum = part_sum + jnp.dot(h_prev, w_rec, preferred_element_type=jnp.float32)
            z_own = lax.psum_scatter(part_sum, "row", scatter_dimension=1, tiled=True) + b_own
            h_own, c_new = gate_update(z_own, c_prev)
            h_next = lax.all_gather(h_own, "col", axis=1, tiled=True)
            return (h_next, c_new), (h_next if keep_rows else h_own)

        return lax.scan(lstm_step, (h_rows, c_own), in_rows)

    def local_program(seq_in, w_in1, w_rec1, b_gate1, w_in2, w_rec2, b_gate2, h_init, c_init):
        unit_dev = b_gate1.shape[0] // 4
        col_index = lax.axis_index("col")

        def own_cells(layer_idx):
            return lax.dynamic_slice_in_dim(c_init[layer_idx], col_index * unit_dev, unit_dev, axis=1)

        carry_one, h1_rows = lstm_layer(seq_in, w_in1, w_rec1, b_gate1, h_init[0].astype(jnp.bfloat16), own_cells(0), True)
        carry_two, h2_own = lstm_layer(h1_rows, w_in2, w_rec2, b_gate2, h_init[1].astype(jnp.bfloat16), own_cells(1), False)
        return h2_own, carry_one[1], carry_two[1]

    row_spec = P(None, "dp", "row")
    weight_spec = P("row", "col")
    bias_spec = P(("col", "row"))
    seq_out_spec = P(None, "dp", ("row", "col"))
    cell_out_spec = P("dp", ("row", "col"))
    return jax.shard_map(
        local_program,
        mesh=mesh,
        in_specs=(row_spec, weight_spec, weight_spec, bias_spec, weight_spec, weight_spec, bias_spec, row_spec, row_spec),
        out_specs=(seq_out_spec, cell_out_spec, cell_out_spec),
        check_vma=False,
    )
```

profile of v0, /device:TPU:0, one launch (start us, length us, event | category | flops | bytes accessed | tf_op | source)
XLA Modules:
  0.0 7669.6 jit_solution(11460404162900939922)
XLA Ops:
  9.2 3861.7 %while.28 = (s32[]{:T(128)}, bf16[32,640]{1,0:T(8,128)(2,1)S(1)}, f32[32,320]{1,0:T(8,128)S(1)}, bf16[128,32,640]{2,1,0:T(8,128)(2,1)}, bf16[128,32,640]{2,1,0:T...) while((s32[]{:T(128)}, bf16[32,640]{1,0:T(8,128)(2,1)S(1)}, ...), condition=%wide.region_2.3_spmd, body=%wide.region_0.2_spmd.sunk | while | flops 419778560 | bytes 44754124 | solution.py:29
  16.1 19.8 reduce-scatter.3.cloned.1.call-done
  169.7 17.0 reduce-scatter.3.cloned.1.call-done
  199.9 17.0 reduce-scatter.3.cloned.1.call-done
  290.3 17.0 reduce-scatter.3.cloned.1.call-done
  652.1 17.0 reduce-scatter.3.cloned.1.call-done
  1074.1 17.0 reduce-scatter.3.cloned.1.call-done
  1134.4 17.0 reduce-scatter.3.cloned.1.call-done
  1285.2 17.0 reduce-scatter.3.cloned.1.call-done
  1375.6 17.0 reduce-scatter.3.cloned.1.call-done
  1496.2 17.0 reduce-scatter.3.cloned.1.call-done
  1797.7 17.0 reduce-scatter.3.cloned.1.call-done
  1948.4 17.0 reduce-scatter.3.cloned.1.call-done
  2069.0 17.0 reduce-scatter.3.cloned.1.call-done
  2189.6 17.0 reduce-scatter.3.cloned.1.call-done
  2370.5 17.0 reduce-scatter.3.cloned.1.call-done
  2641.8 17.0 reduce-scatter.3.cloned.1.call-done
  2762.4 17.0 reduce-scatter.3.cloned.1.call-done
  2883.0 17.0 reduce-scatter.3.cloned.1.call-done
  3576.3 17.0 reduce-scatter.3.cloned.1.call-done
  3606.5 17.0 reduce-scatter.3.cloned.1.call-done
  3727.1 17.0 reduce-scatter.3.cloned.1.call-done
  3871.5 3788.1 %while.29 = (s32[]{:T(128)}, bf16[32,640]{1,0:T(8,128)(2,1)S(1)}, f32[32,320]{1,0:T(8,128)S(1)}, bf16[128,32,320]{2,1,0:T(8,128)(2,1)S(1)}, bf16[128,32,640]{2,1...) while((s32[]{:T(128)}, bf16[32,640]{1,0:T(8,128)(2,1)S(1)}, ...), condition=%wide.region_5.6_spmd, body=%wide.region_3.5_spmd.sunk | while | flops 419778560 | bytes 44729520 | solution.py:29
  4115.2 17.0 reduce-scatter.5.cloned.1.call-done
  4263.1 17.0 reduce-scatter.5.cloned.1.call-done
  4411.1 17.0 reduce-scatter.5.cloned.1.call-done
  4559.1 17.0 reduce-scatter.5.cloned.1.call-done
  4707.1 17.0 reduce-scatter.5.cloned.1.call-done
  5003.0 17.0 reduce-scatter.5.cloned.1.call-done
  5151.0 17.0 reduce-scatter.5.cloned.1.call-done
  5299.0 17.0 reduce-scatter.5.cloned.1.call-done
  5446.9 17.0 reduce-scatter.5.cloned.1.call-done
  (3439 shorter events, 7134.8 us)
Async XLA Ops:
  9.2 26.7 reduce-scatter.3.cloned.1.call-start
  3960.2 23.9 reduce-scatter.5.cloned.1.call-start
  3989.8 23.9 reduce-scatter.5.cloned.1.call-start
  4108.2 23.9 reduce-scatter.5.cloned.1.call-start
  4137.8 23.9 reduce-scatter.5.cloned.1.call-start
  4256.2 23.9 reduce-scatter.5.cloned.1.call-start
  4285.8 23.9 reduce-scatter.5.cloned.1.call-start
  4404.2 23.9 reduce-scatter.5.cloned.1.call-start
  4433.8 23.9 reduce-scatter.5.cloned.1.call-start
  4552.1 23.9 reduce-scatter.5.cloned.1.call-start
  4581.7 23.9 reduce-scatter.5.cloned.1.call-start
  4700.1 23.9 reduce-scatter.5.cloned.1.call-start
  4729.7 23.9 reduce-scatter.5.cloned.1.call-start
  4848.1 23.9 reduce-scatter.5.cloned.1.call-start
  4877.7 23.9 reduce-scatter.5.cloned.1.call-start
  4996.1 23.9 reduce-scatter.5.cloned.1.call-start
  5025.7 23.9 reduce-scatter.5.cloned.1.call-start
  5144.0 23.9 reduce-scatter.5.cloned.1.call-start
  5173.6 23.9 reduce-scatter.5.cloned.1.call-start
  5292.0 23.9 reduce-scatter.5.cloned.1.call-start
  5321.6 23.9 reduce-scatter.5.cloned.1.call-start
  5440.0 23.9 reduce-scatter.5.cloned.1.call-start
  5469.6 23.9 reduce-scatter.5.cloned.1.call-start
  5588.0 23.9 reduce-scatter.5.cloned.1.call-start
  5617.6 23.9 reduce-scatter.5.cloned.1.call-start
  6209.5 23.9 reduce-scatter.5.cloned.1.call-start
  6475.8 23.9 reduce-scatter.5.cloned.1.call-start
  6623.8 23.9 reduce-scatter.5.cloned.1.call-start
  7097.3 23.9 reduce-scatter.5.cloned.1.call-start
  7245.3 23.9 reduce-scatter.5.cloned.1.call-start
  7363.7 23.9 reduce-scatter.5.cloned.1.call-start
  7511.6 23.9 reduce-scatter.5.cloned.1.call-start
  (611 other events, 12929.7 us)
Sparse Core Ops, SparseCore 0:
  16.3 19.5 reduce-scatter.2
  49.2 16.7 reduce-scatter.2
  169.8 16.7 reduce-scatter.2
  200.0 16.7 reduce-scatter.2
  290.4 16.7 reduce-scatter.2
  652.2 16.7 reduce-scatter.2
  1074.2 16.7 reduce-scatter.2
  1104.4 16.7 reduce-scatter.2
  1134.6 16.7 reduce-scatter.2
  1285.3 16.7 reduce-scatter.2
  1375.8 16.7 reduce-scatter.2
  1496.3 16.7 reduce-scatter.2
  1797.8 16.7 reduce-scatter.2
  1948.5 16.7 reduce-scatter.2
  2069.1 16.7 reduce-scatter.2
  2189.7 16.7 reduce-scatter.2
  2370.6 16.7 reduce-scatter.2
  2641.9 16.7 reduce-scatter.2
  2762.5 16.7 reduce-scatter.2
  2883.1 16.7 reduce-scatter.2
  3576.5 16.7 reduce-scatter.2
  3606.6 16.7 reduce-scatter.2
  3727.2 16.7 reduce-scatter.2
  4115.3 16.7 reduce-scatter.4
  4263.2 16.7 reduce-scatter.4
  4411.2 16.7 reduce-scatter.4
  4559.2 16.7 reduce-scatter.4
  4707.2 16.7 reduce-scatter.4
  4855.1 16.7 reduce-scatter.4
  5003.1 16.7 reduce-scatter.4
  5151.1 16.7 reduce-scatter.4
  5299.1 16.7 reduce-scatter.4
  (224 shorter events, 3744.2 us)
where the time goes:
time: 7680 us; the launch traced here: 7670 us
  waiting for transfers between devices  4340 us (57%)
  matrix products  1630 us (21%)
  blocking collectives  1150 us (15%)
  other arithmetic  271 us (4%)
  local copies, waits for them, and re-layouts  242 us (3%)
    reduce_scatter x256, waiting for transfers between devices, lstm_step(): lax.psum_scatter(part_sum, 'row', scatter_dimension=1, tiled=True) + b_own  4340 us
    all_gather x256, blocking collectives, lstm_step(): h_next = lax.all_gather(h_own, 'col', axis=1, tiled=True)  1150 us
    dot_general x256, matrix products, lstm_step(): part_sum = jnp.dot(in_step, w_in, preferred_element_type=jnp.float32)  1090 us
    dot_general x256, matrix products, lstm_step(): jnp.dot(h_prev, w_rec, preferred_element_type=jnp.float32)  540 us
    add x256, other arithmetic, lstm_step(): lax.psum_scatter(part_sum, 'row', scatter_dimension=1, tiled=True) + b_own  238 us
  transfers between devices with their start and end apart: 256, of which 256 were waited for; matrix products, arithmetic and copies ran while one was open for 0% of the time, Pallas kernels for 0%

commit v1 on v0

v1 whole, which is shorter than its diff:
```python
import jax
import jax.numpy as jnp
from jax import lax
from jax.experimental import pallas as pl
from jax.experimental.pallas import tpu as pltpu
from jax.sharding import PartitionSpec as P

MESH = pl.DeviceIdType.MESH
F32, BF16 = jnp.float32, jnp.bfloat16
LANES = 128
TILE = 256
STEPS, BATCH, HIDDEN = 128, 32, 2560
UNIT = 320
CHIP = 2 * UNIT
GATES = 4 * CHIP
TB = 4
NBLK = STEPS // TB
ROWS = TB * BATCH
LEAD = 3
NCHUNK = CHIP // LANES
MAIN = 2 * TILE
REST = CHIP - MAIN
CW = 4 * LANES
SHARE = ((0, 1, 2), (3, 4, 5), (6, 7), (8, 9))
PAD = 3 * LANES
FILL = 96
PARTNER, ACROSS, OVER = (0, 1, 0), (1, 0, 0), (1, 1, 0)
PEERS = ((1, 0, 1), (1, 0, 0), (0, 0, 1))
DIAG, NEXT_X, NEXT_Y = range(3)


def _roll_half(v):
    return pltpu.roll(v, LANES // 2, 1)


def _low_half(v):
    return lax.broadcasted_iota(jnp.int32, v.shape, 1) < LANES // 2


def _halves(get, first, second):
    if first % 2 == 0 and second == first + 1:
        return get(first // 2)
    lo, hi = get(first // 2), get(second // 2)
    lo = lo if first % 2 == 0 else _roll_half(lo)
    hi = hi if second % 2 == 1 else _roll_half(hi)
    return jnp.where(_low_half(lo), lo, hi)


def _repack(get, put):
    for chunk in range(NCHUNK):
        for gate in range(4):
            place = [20 * (u // 5) + 5 * gate + u % 5 for u in (2 * chunk, 2 * chunk + 1)]
            put(4 * chunk + gate, _halves(get, *place))


def _sigmoid(v):
    return 0.5 * jnp.tanh(0.5 * v) + 0.5


def _kernel(
    seq, w_in1, w_rec1, w_in2, w_rec2, bias, hc, h2_out, c1_out, c2_out, stage,
    win, wrec, a8, a4, zbuf, z, h8, h4, c_s, bias_s, braw, hcraw, out_own, out_far, size,
    w_recv, w_send, st_recv, st_send, fw_send, small_recv, small_send, seq_recv, seq_send, a_recv,
    h_recv, h_send, d_send, o_recv, o_send, c_recv, c_send,
):
    col, row = lax.axis_index("col"), lax.axis_index("row")
    x, core = row // 2, lax.rem(row, 2)

    def device(dx, dcore, dcol):
        px, pc, py = lax.rem(x + dx, 2), lax.rem(core + dcore, 2), lax.rem(col + dcol, 2)
        return {"col": py, "row": 2 * px + pc}

    def remote(src, dst, send, recv, to):
        return pltpu.make_async_remote_copy(
            src_ref=src, dst_ref=dst, send_sem=send, recv_sem=recv, device_id=device(*to), device_id_type=MESH
        )

    def arrived(ref, sem):
        pltpu.make_async_copy(ref, ref, sem).wait()

    def units_moved(units, sem):
        arrived(size.at[pl.ds(0, units // 8)], sem)

    barrier = pltpu.get_barrier_semaphore()
    others = [(dx, dc, dy) for dx in range(2) for dc in range(2) for dy in range(2) if dx + dc + dy]
    for to in others:
        pl.semaphore_signal(barrier, inc=1, device_id=device(*to), device_id_type=MESH)
    pl.semaphore_wait(barrier, len(others))

    own_cols = pl.ds(pl.multiple_of(x * GATES, GATES), GATES)
    far_cols = pl.ds(pl.multiple_of((1 - x) * GATES, GATES), GATES)

    def pieces(by_unit, src_core, half):
        start = half * UNIT
        unit = src_core * UNIT if by_unit else start
        whole = min(UNIT, MAIN - unit)
        out = [(start, whole, unit)]
        if whole < UNIT:
            out.append((start + whole, UNIT - whole, MAIN))
        return out

    def place(by_unit, cross, src_core, half, unit):
        group = cross + 2 * jnp.where(half == col, 0, 1) if by_unit else 2 * cross + src_core
        off = group * MAIN + unit if unit < MAIN else MAIN * 4 + group * REST
        return pl.multiple_of(off, 64)

    def w_copies(mat, by_unit, src_core, ref, cross, cols, buf, to, send_base):
        out = []
        for half in range(2):
            for i, (start, rows, unit) in enumerate(pieces(by_unit, src_core, half)):
                src = ref.at[pl.ds(start, rows), cols]
                dst = buf.at[pl.ds(place(by_unit, cross, src_core, half, unit), rows), :]
                recv = w_recv.at[mat, cross, src_core, half, i]
                if to is None:
                    out.append(pltpu.make_async_copy(src, dst, recv))
                else:
                    out.append(remote(src, dst, w_send.at[send_base + half, i], recv, to))
        return out

    def take_weights(buf, by_unit, mat, cross, src_core):
        for half in range(2):
            for i, (_, count, unit) in enumerate(pieces(by_unit, src_core, half)):
                off = place(by_unit, cross, src_core, half, unit)
                arrived(buf.at[pl.ds(off, count), :], w_recv.at[mat, cross, src_core, half, i])

                def group(g, carry):
                    rows = pl.ds(pl.multiple_of(off + g * 16, 16), 16)
                    tiles = [buf[rows, pl.ds(LANES * n, LANES)].astype(F32) for n in range(GATES // LANES)]

                    def put(n, v):
                        buf[rows, pl.ds(LANES * n, LANES)] = v.astype(BF16)

                    _repack(lambda n: tiles[n], put)
                    return carry

                lax.fori_loop(0, count // 16, group, 0)

    def tiles_of(buf8, buf4, at, ks):
        out = [buf8[at, k] if k < 8 else buf4[at, 2 * (k - 8) + i] for k in ks for i in range(1 if k < 8 else 2)]
        return jnp.concatenate(out, axis=1)

    def rows_of(weights, ks, j):
        cols = pl.ds(CW * j, CW)
        if list(ks) == list(range(ks[0], ks[0] + len(ks))):
            return weights[pl.ds(TILE * ks[0], TILE * len(ks)), cols]
        return jnp.concatenate([weights[pl.ds(TILE * k, TILE), cols] for k in ks], axis=0)

    def rec_dot(slot, ks, j):
        rows = jnp.concatenate([tiles_of(h8, h4, slot, ks), jnp.zeros((FILL, TILE * len(ks)), BF16)], axis=0)
        return jnp.dot(rows, rows_of(wrec, ks, j), preferred_element_type=F32)[:BATCH]

    def in_product(block, into, ks):
        for j in range(NCHUNK):
            cols = pl.ds(CW * j, CW)
            part = jnp.dot(tiles_of(a8, a4, block, ks), rows_of(win, ks, j), preferred_element_type=F32)
            if ks[0] == 0:
                zbuf[into, :, cols] = part + bias_s[0:1, cols]
            else:
                zbuf[into, :, cols] += part

    def put_h(slot, chunk, v):
        if chunk < 4:
            h8[slot, chunk // 2, :, pl.ds(LANES * (chunk % 2), LANES)] = v.astype(BF16)
        else:
            h4[slot, 0] = v.astype(BF16)

    def small_setup():
        for i in range(2):
            arrived(braw.at[i], small_recv.at[0, i])
            arrived(hcraw.at[i], small_recv.at[1, i])

        def put_bias(n, v):
            bias_s[:, pl.ds(LANES * n, LANES)] = v

        _repack(lambda n: braw[n // 10, :, pl.ds(LANES * (n % 10), LANES)], put_bias)
        for which in range(2):
            def get(n):
                return hcraw[n // 3, which, :, pl.ds(LANES * (n % 3), LANES)]

            for chunk in range(NCHUNK):
                v = _halves(get, *[u + u // 5 for u in (2 * chunk, 2 * chunk + 1)])
                if which == 0:
                    put_h(TB - 1, chunk, v)
                else:
                    c_s[:, pl.ds(LANES * chunk, LANES)] = v

    def split_units(get):
        near = [get(0), get(1), get(2)]
        a, b, c = (_roll_half(get(n)) for n in (2, 3, 4))
        return near, [jnp.where(_low_half(a), a, b), jnp.where(_low_half(b), b, c), c]

    def h_copy(slot, peer, part):
        to = PEERS[peer]
        rel = to[0] + 2 * to[2]
        if part < 2:
            src, dst = h8.at[slot, part], h8.at[slot, 2 * rel + part]
        else:
            src, dst = h4.at[slot, 0], h4.at[slot, rel]
        return remote(src, dst, h_send.at[slot], h_recv.at[slot, peer, part], to)

    def send_h(slot, part):
        for peer in range(3):
            h_copy(slot, peer, part).start()

    def h_sent(slot):
        units_moved(3 * CHIP, h_send.at[slot])

    def pass_on(block, s, slot):
        rows = pl.ds(BATCH * s, BATCH)
        return (
            remote(h8.at[slot], a8.at[block, :, rows, :], d_send.at[slot], a_recv.at[block], PARTNER),
            remote(h4.at[slot], a4.at[block, :, rows, :], d_send.at[slot], a_recv.at[block], PARTNER),
        )

    def passed_on(slot):
        units_moved(HIDDEN, d_send.at[slot])

    def seq_pieces(block, i, send):
        out = [remote(a8.at[block, i], a8.at[block, 4 + i], seq_send.at[send], a_recv.at[block], ACROSS)]
        if i < 2:
            out.append(remote(a4.at[block, i], a4.at[block, 2 + i], seq_send.at[send], a_recv.at[block], ACROSS))
        return out

    def seq_sent(i, send):
        units_moved(TB * (TILE + LANES if i < 2 else TILE), seq_send.at[send])

    def wait_block(layer, block):
        units_moved(TB * (HIDDEN if layer else HIDDEN // 2), a_recv.at[block])

    def out_copies(block, ring):
        return (
            pltpu.make_async_copy(out_own.at[ring], h2_out.at[block], o_send.at[ring, 0]),
            remote(out_far.at[ring], h2_out.at[block], o_send.at[ring, 1], o_recv, PARTNER),
        )

    def out_wait(block, ring):
        own, far = out_copies(block, ring)
        own.wait()
        far.wait_send()

    def one_step(layer, b, s):
        prev = (s + TB - 1) % TB
        ring = lax.rem(b, 2)
        nxt = jnp.minimum(b + 1, NBLK - 1)
        rows = pl.ds(BATCH * s, BATCH)

        def wait_for(*parts):
            for peer, part in parts:
                h_copy(prev, peer, part).wait_recv()

        for j in range(NCHUNK):
            cols = pl.ds(CW * j, CW)
            z[:, cols] = zbuf[ring, rows, cols] + rec_dot(prev, (0, 1), j)
        if s == 0:
            @pl.when(b + 1 < NBLK)
            def _():
                wait_block(layer, nxt)
        in_product(nxt, 1 - ring, SHARE[s])
        if layer == 0:
            @pl.when(b + LEAD < NBLK)
            def _():
                for cp in seq_pieces(jnp.minimum(b + LEAD, NBLK - 1), s, s):
                    cp.start()
        wait_for((NEXT_Y, 0), (NEXT_X, 0), (NEXT_Y, 1))
        for j in range(NCHUNK):
            z[:, pl.ds(CW * j, CW)] += rec_dot(prev, (4, 5, 2), j)
        wait_for((DIAG, 0), (NEXT_X, 1), (NEXT_Y, 2), (NEXT_X, 2), (DIAG, 1), (DIAG, 2))
        if layer == 0:
            if s == 0:
                @pl.when(b > 0)
                def _():
                    for cp in pass_on(jnp.maximum(b - 1, 0), TB - 1, prev):
                        cp.start()
            else:
                for cp in pass_on(b, s - 1, prev):
                    cp.start()
        if s == TB - 1:
            h_sent(s)
        else:
            pl.when(b > 0)(lambda: h_sent(s))
        if layer == 0:
            if s == TB - 1:
                passed_on(0)
            else:
                pl.when(b > 0)(lambda: passed_on((s + 1) % TB))
        if layer == 1 and s == 0:
            pl.when(b > 1)(lambda: out_wait(jnp.maximum(b - 2, 0), ring))

        new, part = [], []

        def products(*chunks):
            for j in chunks:
                part.append(rec_dot(prev, (6, 3, 7, 8, 9), j))

        def cell(j):
            units = pl.ds(LANES * j, LANES)
            zj = z[:, pl.ds(CW * j, CW)] + part[j]
            gates = [zj[:, LANES * m : LANES * (m + 1)] for m in range(4)]
            c_new = _sigmoid(gates[1]) * c_s[:, units] + _sigmoid(gates[0]) * jnp.tanh(gates[2])
            c_s[:, units] = c_new
            h_new = _sigmoid(gates[3]) * jnp.tanh(c_new)
            new.append(h_new)
            put_h(s, j, h_new)

        products(0, 1, 2)
        cell(0)
        cell(1)
        send_h(s, 0)
        products(3, 4)
        cell(2)
        cell(3)
        send_h(s, 1)
        cell(4)
        send_h(s, 2)
        if layer == 1:
            near, far = split_units(lambda n: new[n])
            for n in range(3):
                out_far[ring, rows, pl.ds(LANES * n, LANES)] = near[n].astype(BF16)
                out_own[ring, rows, pl.ds(LANES * n, LANES)] = far[n].astype(BF16)
            if s == TB - 1:
                for cp in out_copies(b, ring):
                    cp.start()

    def run_layer(layer):
        for ks in SHARE:
            in_product(0, 0, ks)

        def block(b, carry):
            if layer == 0:
                @pl.when((b > 0) & (b + LEAD - 1 < NBLK))
                def _():
                    for s in range(TB):
                        seq_sent(s, s)
            for s in range(TB):
                one_step(layer, b, s)
            return carry

        lax.fori_loop(0, NBLK, block, 0)
        slot = TB - 1
        for peer in range(3):
            for part in range(3):
                h_copy(slot, peer, part).wait_recv()
        if layer == 0:
            for cp in pass_on(NBLK - 1, slot, slot):
                cp.start()
            for s in (1, 2, 3):
                passed_on(s)
        for s in range(TB):
            h_sent(s)

    def begin():
        small_setup()
        for part in range(3):
            send_h(TB - 1, part)

    def end(keep, give, out, other):
        parts = split_units(lambda n: c_s[:, pl.ds(LANES * n, LANES)])
        for i in range(2):
            for n in range(3):
                hcraw[0, i, :, pl.ds(LANES * n, LANES)] = parts[i][n]
        kept = pltpu.make_async_copy(hcraw.at[0, keep], out, c_send.at[0])
        given = remote(hcraw.at[0, give], out, c_send.at[1], c_recv, PARTNER)
        kept.start()
        given.start()
        kept.wait()
        given.wait_send()
        arrived(other, c_recv)

    def seq_copies(group, rel, to, sems):
        out = []
        for i in range(3):
            src = seq.at[:, :, pl.ds(TILE * i, TILE if i < 2 else REST)]
            dst = a8.at[:, 2 * rel + i] if i < 2 else a4.at[:, rel]
            if to is None:
                out.append(pltpu.make_async_copy(src, dst, seq_recv.at[rel, i]))
            else:
                out.append(remote(src, dst, sems[i], seq_recv.at[rel, i], to))
        return out

    @pl.when(core == 0)
    def _():
        local = seq_copies(0, 0, None, None)
        local.append(pltpu.make_async_copy(bias.at[0], braw.at[0], small_recv.at[0, 0]))
        local.append(pltpu.make_async_copy(hc.at[0], hcraw.at[0], small_recv.at[1, 0]))
        local += w_copies(0, False, 0, w_in1, 0, own_cols, win, None, 0)
        local += w_copies(1, True, 0, w_rec1, 0, own_cols, wrec, None, 0)
        sent = [
            remote(bias.at[1], braw.at[0], small_send.at[0], small_recv.at[0, 0], PARTNER),
            remote(hc.at[1], hcraw.at[0], small_send.at[1], small_recv.at[1, 0], PARTNER),
            remote(w_in2.at[:, far_cols], stage.at[0], st_send.at[0], st_recv.at[0], PARTNER),
            remote(w_rec2.at[:, far_cols], stage.at[1], st_send.at[1], st_recv.at[1], PARTNER),
        ]
        sent += w_copies(0, True, 0, w_in2, 0, own_cols, win, PARTNER, 4)
        sent += w_copies(1, True, 0, w_rec2, 0, own_cols, wrec, PARTNER, 6)
        cross_in = w_copies(0, False, 0, w_in1, 1, far_cols, win, ACROSS, 0)
        cross_rec = w_copies(1, True, 0, w_rec1, 1, far_cols, wrec, ACROSS, 2)
        for cp in cross_in + local + sent:
            cp.start()
        for rel in range(2):
            for i in range(3):
                arrived(a8.at[:, 2 * rel + i] if i < 2 else a4.at[:, rel], seq_recv.at[rel, i])
        for b in range(LEAD):
            for i in range(TB):
                for cp in seq_pieces(b, i, TB + TB * b + i):
                    cp.start()
        for cp in cross_rec:
            cp.start()
        begin()
        for mat, buf in enumerate((win, wrec)):
            for cross in range(2):
                for src_core in range(2):
                    take_weights(buf, mat == 1, mat, cross, src_core)
        wait_block(0, 0)
        run_layer(0)
        end(0, 1, c1_out, c2_out)
        arrived(h2_out, o_recv)
        for b in range(LEAD):
            for i in range(TB):
                seq_sent(i, TB + TB * b + i)
        for cp in sent + cross_in + cross_rec:
            cp.wait_send()

    @pl.when(core == 1)
    def _():
        local = [
            pltpu.make_async_copy(bias.at[1], braw.at[1], small_recv.at[0, 1]),
            pltpu.make_async_copy(hc.at[1], hcraw.at[1], small_recv.at[1, 1]),
        ]
        local += w_copies(0, True, 1, w_in2, 0, own_cols, win, None, 0)
        local += w_copies(1, True, 1, w_rec2, 0, own_cols, wrec, None, 0)
        sent = seq_copies(0, 1, PARTNER, [small_send.at[2 + i] for i in range(3)])
        sent.append(remote(bias.at[0], braw.at[1], small_send.at[0], small_recv.at[0, 1], PARTNER))
        sent.append(remote(hc.at[0], hcraw.at[1], small_send.at[1], small_recv.at[1, 1], PARTNER))
        sent += w_copies(0, False, 1, w_in1, 1, far_cols, win, OVER, 0)
        sent += w_copies(1, True, 1, w_rec1, 1, far_cols, wrec, OVER, 2)
        sent += w_copies(0, False, 1, w_in1, 0, own_cols, win, PARTNER, 4)
        sent += w_copies(1, True, 1, w_rec1, 0, own_cols, wrec, PARTNER, 6)
        late_rec = w_copies(1, True, 1, w_rec2, 1, far_cols, wrec, ACROSS, 10)
        for cp in sent + local:
            cp.start()
        late = w_copies(0, True, 1, w_in2, 1, far_cols, win, ACROSS, 8)
        for mat, buf, more in ((0, win, late_rec), (1, wrec, [])):
            arrived(stage.at[mat], st_recv.at[mat])
            for half in range(2):
                rows = pl.ds(place(True, 1, 0, half, 0), UNIT)
                src = stage.at[mat, pl.ds(half * UNIT, UNIT), :]
                late.append(remote(src, buf.at[rows, :], fw_send.at[mat, half], w_recv.at[mat, 1, 0, half, 0], ACROSS))
            late += more
        for cp in late:
            cp.start()
        begin()
        for mat, buf in enumerate((win, wrec)):
            for cross in range(2):
                for src_core in (1, 0):
                    take_weights(buf, True, mat, cross, src_core)
        wait_block(1, 0)
        run_layer(1)
        for b in (NBLK - 2, NBLK - 1):
            out_wait(b, b % 2)
        end(1, 0, c2_out, c1_out)
        for cp in sent + late:
            cp.wait_send()


def solution(mesh):
    any_spec = pl.BlockSpec(memory_space=pl.ANY)
    dma = pltpu.SemaphoreType.DMA
    vmem = pltpu.VMEM

    def local_program(seq_in, w_in1, w_rec1, b_gate1, w_in2, w_rec2, b_gate2, h_init, c_init):
        col = lax.axis_index("col")
        states = jnp.stack([h_init, c_init], axis=1)
        states = lax.dynamic_slice_in_dim(states, col * UNIT, UNIT, axis=3)
        states = jnp.pad(states, ((0, 0), (0, 0), (0, 0), (0, PAD - UNIT)))
        bias = jnp.broadcast_to(jnp.stack([b_gate1, b_gate2])[:, None, :], (2, 8, 4 * UNIT))
        seq = seq_in.reshape(NBLK, ROWS, CHIP)
        h2, c1, c2, _ = pl.pallas_call(
            _kernel,
            out_shape=(
                jax.ShapeDtypeStruct((NBLK, ROWS, PAD), BF16),
                jax.ShapeDtypeStruct((BATCH, PAD), F32),
                jax.ShapeDtypeStruct((BATCH, PAD), F32),
                jax.ShapeDtypeStruct((2, CHIP, GATES), BF16),
            ),
            in_specs=[any_spec] * 7,
            out_specs=(any_spec,) * 4,
            scratch_shapes=[
                vmem((HIDDEN, GATES), BF16),
                vmem((HIDDEN, GATES), BF16),
                vmem((NBLK, 8, ROWS, TILE), BF16),
                vmem((NBLK, 4, ROWS, LANES), BF16),
                vmem((2, ROWS, GATES), F32),
                vmem((BATCH, GATES), F32),
                vmem((TB, 8, BATCH, TILE), BF16),
                vmem((TB, 4, BATCH, LANES), BF16),
                vmem((BATCH, CHIP), F32),
                vmem((8, GATES), F32),
                vmem((2, 8, 4 * UNIT), F32),
                vmem((2, 2, BATCH, PAD), F32),
                vmem((2, ROWS, PAD), BF16),
                vmem((2, ROWS, PAD), BF16),
                vmem((TB * HIDDEN // 8, LANES), F32),
                dma((2, 2, 2, 2, 2)),
                dma((12, 2)),
                dma((2,)),
                dma((2,)),
                dma((2, 2)),
                dma((2, 2)),
                dma((5,)),
                dma((2, 3)),
                dma((TB + TB * LEAD,)),
                dma((NBLK,)),
                dma((TB, 3, 3)),
                dma((TB,)),
                dma((TB,)),
                dma(()),
                dma((2, 2)),
                dma(()),
                dma((2,)),
            ],
            compiler_params=pltpu.CompilerParams(
                collective_id=0, has_side_effects=True, vmem_limit_bytes=62 * 2**20
            ),
        )(seq, w_in1, w_rec1, w_in2, w_rec2, bias, states)
        return h2.reshape(STEPS, BATCH, PAD)[:, :, :UNIT], c1[:, :UNIT], c2[:, :UNIT]

    row_spec = P(None, "dp", "row")
    weight_spec = P("row", "col")
    bias_spec = P(("col", "row"))
    seq_out_spec = P(None, "dp", ("row", "col"))
    cell_out_spec = P("dp", ("row", "col"))
    return jax.shard_map(
        local_program,
        mesh=mesh,
        in_specs=(row_spec, weight_spec, weight_spec, bias_spec, weight_spec, weight_spec, bias_spec, row_spec, row_spec),
        out_specs=(seq_out_spec, cell_out_spec, cell_out_spec),
        check_vma=False,
    )
```

time: 7680 us -> 888 us (0.12)
  waiting for transfers between devices: 4340 us -> 0 us
  matrix products: 1630 us -> 0 us
  blocking collectives: 1150 us -> 0 us
  Pallas kernels: 0 us -> 876 us
  other arithmetic: 271 us -> 1.09 us
  local copies, waits for them, and re-layouts: 242 us -> 10.4 us
    reduce_scatter x256 -> x0, waiting for transfers between devices: 4340 us -> none  [lstm_step(): lax.psum_scatter(part_sum, 'row', scatter_dimension=1, tiled=True) + b_own]
    dot_general x512 -> x0, matrix products: 1630 us -> none  [the longest x256 1090 us: lstm_step(): part_sum = jnp.dot(in_step, w_in, preferred_element_type=jnp.float32)]
    all_gather x256 -> x0, blocking collectives: 1150 us -> none  [lstm_step(): h_next = lax.all_gather(h_own, 'col', axis=1, tiled=True)]
    pallas_call x0 -> x1, Pallas kernels: none -> 876 us  [local_program(): pl.pallas_call(_kernel, out_shape=(jax.ShapeDtypeStruct((NBLK, ROWS, PAD)...]
    add x256 -> x0, other arithmetic: 238 us -> none  [lstm_step(): lax.psum_scatter(part_sum, 'row', scatter_dimension=1, tiled=True) + b_own]
    while x1024 -> x0, local copies, waits for them, and re-layouts: 148 us -> none
    dynamic_update_slice x128 -> x0, local copies, waits for them, and re-layouts: 79.6 us -> none  [lstm_layer(): return lax.scan(lstm_step, (h_rows, c_own), in_rows)]
  transfers between devices with their start and end apart: 256 -> 0, of which waited for: 256 -> 0; matrix products, arithmetic and copies ran while one was open for 0% -> 0% of each run, Pallas kernels for 0% -> 0%
where the time goes in v1:
time: 888 us
  Pallas kernels  876 us (99%)
  local copies, waits for them, and re-layouts  10.4 us (1%)
    pallas_call x1, Pallas kernels, local_program(): pl.pallas_call(_kernel, out_shape=(jax.ShapeDtypeStruct((NBLK, ROWS, PAD)...  876 us

profile of v1, /device:TPU:0, one launch (start us, length us, event | category | flops | bytes accessed | tf_op | source)
XLA Modules:
  0.0 887.9 jit_solution(152705147406952593)
XLA Ops:
  0.6 0.7 stack.18
  1.3 0.7 stack.19
  2.1 0.6 broadcast_in_dim.2.bias
  2.7 1.1 fusion
  3.8 0.7 pad.4.hc
  4.5 875.8 %shard_map.112 = (bf16[32,128,384]{2,1,0:T(8,128)(2,1)}, f32[32,384]{1,0:T(8,128)}, f32[32,384]{1,0:T(8,128)}, bf16[2,640,2560]{2,1,0:T(8,128)(2,1)}) custom-call(bf16[32,128,640]{2,1,0:T(8,128)(2,1)} %bitcast.7, bf16[640,5120]{1,0:T(8,128)(2,1)} %w_in1.1, bf16[640,5120]{1,0:T(8,128)(2,1)} %w_rec1.1, bf16[640,5120]{1,0:T(8,128)(2,1)} %w_in2.1, ...), custom_call_target="tpu_custom_call" | custom-call | tf_op jit(solution)/shard_map/pallas_call | solution.py:477
  880.3 4.8 copy.13
  885.1 1.4 copy.16
  886.5 1.4 copy.17
  (1 shorter events, 0.0 us)

commit v2 on v1

--- a/solution.py
+++ b/solution.py
@@ -17,6 +17,7 @@
 NBLK = STEPS // TB
 ROWS = TB * BATCH
 LEAD = 3
+DIRECT = ((0, 0),)
 NCHUNK = CHIP // LANES
 MAIN = 2 * TILE
 REST = CHIP - MAIN
@@ -24,7 +25,7 @@
 SHARE = ((0, 1, 2), (3, 4, 5), (6, 7), (8, 9))
 PAD = 3 * LANES
 FILL = 96
-PARTNER, ACROSS, OVER = (0, 1, 0), (1, 0, 0), (1, 1, 0)
+PARTNER, ACROSS, OVER, ALONG = (0, 1, 0), (1, 0, 0), (1, 1, 0), (0, 0, 1)
 PEERS = ((1, 0, 1), (1, 0, 0), (0, 0, 1))
 DIAG, NEXT_X, NEXT_Y = range(3)
 
@@ -58,7 +59,7 @@
 
 
 def _kernel(
-    seq, w_in1, w_rec1, w_in2, w_rec2, bias, hc, h2_out, c1_out, c2_out, stage,
+    seq, w_in1, w_rec1, w_in2, w_rec2, bias1, bias2, h_first, c_first, h2_out, c1_out, c2_out, stage,
     win, wrec, a8, a4, zbuf, z, h8, h4, c_s, bias_s, braw, hcraw, out_own, out_far, size,
     w_recv, w_send, st_recv, st_send, fw_send, small_recv, small_send, seq_recv, seq_send, a_recv,
     h_recv, h_send, d_send, o_recv, o_send, c_recv, c_send,
@@ -133,7 +134,7 @@
                     _repack(lambda n: tiles[n], put)
                     return carry
 
-                lax.fori_loop(0, count // 16, group, 0)
+                lax.fori_loop(0, count // 16, group, 0, unroll=4)
 
     def tiles_of(buf8, buf4, at, ks):
         out = [buf8[at, k] if k < 8 else buf4[at, 2 * (k - 8) + i] for k in ks for i in range(1 if k < 8 else 2)]
@@ -165,24 +166,43 @@
             h4[slot, 0] = v.astype(BF16)
 
     def small_setup():
-        for i in range(2):
-            arrived(braw.at[i], small_recv.at[0, i])
-            arrived(hcraw.at[i], small_recv.at[1, i])
+        for src_core in range(2):
+            for i, ref in enumerate((braw.at[src_core], hcraw.at[src_core, 0], hcraw.at[src_core, 1])):
+                arrived(ref, small_recv.at[src_core, i])
+
+        def get_bias(n):
+            return jnp.broadcast_to(braw[n // 10, pl.ds(n % 10, 1), :], (8, LANES))
 
         def put_bias(n, v):
             bias_s[:, pl.ds(LANES * n, LANES)] = v
 
-        _repack(lambda n: braw[n // 10, :, pl.ds(LANES * (n % 10), LANES)], put_bias)
+        _repack(get_bias, put_bias)
         for which in range(2):
             def get(n):
-                return hcraw[n // 3, which, :, pl.ds(LANES * (n % 3), LANES)]
+                return hcraw[n // NCHUNK, which, :, pl.ds(LANES * (n % NCHUNK), LANES)]
 
             for chunk in range(NCHUNK):
-                v = _halves(get, *[u + u // 5 for u in (2 * chunk, 2 * chunk + 1)])
+                blocks = [10 * (u // 5) + u % 5 for u in (2 * chunk, 2 * chunk + 1)]
+                v = jnp.where(col == 0, _halves(get, *blocks), _halves(get, *[n + 5 for n in blocks]))
                 if which == 0:
                     put_h(TB - 1, chunk, v)
                 else:
                     c_s[:, pl.ds(LANES * chunk, LANES)] = v
+
+    def small_copies(layer, src_core, to):
+        refs = (
+            ((bias1, bias2)[layer], braw.at[src_core]),
+            (h_first.at[layer], hcraw.at[src_core, 0]),
+            (c_first.at[layer], hcraw.at[src_core, 1]),
+        )
+        out = []
+        for i, (src, dst) in enumerate(refs):
+            recv = small_recv.at[src_core, i]
+            if to is None:
+                out.append(pltpu.make_async_copy(src, dst, recv))
+            else:
+                out.append(remote(src, dst, small_send.at[i], recv, to))
+        return out
 
     def split_units(get):
         near = [get(0), get(1), get(2)]
@@ -199,8 +219,13 @@
         return remote(src, dst, h_send.at[slot], h_recv.at[slot, peer, part], to)
 
     def send_h(slot, part):
-        for peer in range(3):
-            h_copy(slot, peer, part).start()
+        queue = (
+            ((DIAG, 0), (NEXT_X, 0), (NEXT_Y, 0)),
+            ((DIAG, 1), (NEXT_Y, 1)),
+            ((DIAG, 2), (NEXT_X, 1), (NEXT_X, 2), (NEXT_Y, 2)),
+        )
+        for peer, piece in queue[part]:
+            h_copy(slot, peer, piece).start()
 
     def h_sent(slot):
         units_moved(3 * CHIP, h_send.at[slot])
@@ -215,17 +240,44 @@
     def passed_on(slot):
         units_moved(HIDDEN, d_send.at[slot])
 
-    def seq_pieces(block, i, send):
-        out = [remote(a8.at[block, i], a8.at[block, 4 + i], seq_send.at[send], a_recv.at[block], ACROSS)]
-        if i < 2:
-            out.append(remote(a4.at[block, i], a4.at[block, 2 + i], seq_send.at[send], a_recv.at[block], ACROSS))
-        return out
+    def seq_pieces(block, i, send, hand_on):
+        first, to = (1, ALONG) if hand_on else (0, ACROSS)
+        bufs = ((a8, 4 * first + i, 4 + i), (a4, 2 * first + i, 2 + i))
+        return [
+            remote(buf.at[block, src], buf.at[block, dst], seq_send.at[send], a_recv.at[block], to)
+            for buf, src, dst in bufs[: 2 if i < 2 else 1]
+        ]
+
+    def crosses_here(block):
+        return lax.rem(block + col, 2) == 0
+
+    def seq_step(b, s):
+        ahead, behind = b + LEAD + 1, b + LEAD
+
+        @pl.when(crosses_here(ahead) & (ahead < NBLK))
+        def _():
+            for cp in seq_pieces(jnp.minimum(ahead, NBLK - 1), s, s, False):
+                cp.start()
+
+        @pl.when(crosses_here(behind) & (behind < NBLK))
+        def _():
+            block = jnp.minimum(behind, NBLK - 1)
+            if s == 0:
+                block_arrived(0, block)
+            for cp in seq_pieces(block, s, s, True):
+                cp.start()
 
     def seq_sent(i, send):
         units_moved(TB * (TILE + LANES if i < 2 else TILE), seq_send.at[send])
 
+    def block_arrived(layer, block):
+        units_moved(TB * (HIDDEN if layer else HIDDEN // 2), a_recv.at[block])
+
     def wait_block(layer, block):
-        units_moved(TB * (HIDDEN if layer else HIDDEN // 2), a_recv.at[block])
+        if layer == 0:
+            pl.when(jnp.logical_not(crosses_here(block)))(lambda: block_arrived(layer, block))
+        else:
+            block_arrived(layer, block)
 
     def out_copies(block, ring):
         return (
@@ -248,32 +300,6 @@
             for peer, part in parts:
                 h_copy(prev, peer, part).wait_recv()
 
-        for j in range(NCHUNK):
-            cols = pl.ds(CW * j, CW)
-            z[:, cols] = zbuf[ring, rows, cols] + rec_dot(prev, (0, 1), j)
-        if s == 0:
-            @pl.when(b + 1 < NBLK)
-            def _():
-                wait_block(layer, nxt)
-        in_product(nxt, 1 - ring, SHARE[s])
-        if layer == 0:
-            @pl.when(b + LEAD < NBLK)
-            def _():
-                for cp in seq_pieces(jnp.minimum(b + LEAD, NBLK - 1), s, s):
-                    cp.start()
-        wait_for((NEXT_Y, 0), (NEXT_X, 0), (NEXT_Y, 1))
-        for j in range(NCHUNK):
-            z[:, pl.ds(CW * j, CW)] += rec_dot(prev, (4, 5, 2), j)
-        wait_for((DIAG, 0), (NEXT_X, 1), (NEXT_Y, 2), (NEXT_X, 2), (DIAG, 1), (DIAG, 2))
-        if layer == 0:
-            if s == 0:
-                @pl.when(b > 0)
-                def _():
-                    for cp in pass_on(jnp.maximum(b - 1, 0), TB - 1, prev):
-                        cp.start()
-            else:
-                for cp in pass_on(b, s - 1, prev):
-                    cp.start()
         if s == TB - 1:
             h_sent(s)
         else:
@@ -285,12 +311,31 @@
                 pl.when(b > 0)(lambda: passed_on((s + 1) % TB))
         if layer == 1 and s == 0:
             pl.when(b > 1)(lambda: out_wait(jnp.maximum(b - 2, 0), ring))
-
+        for j in range(NCHUNK):
+            cols = pl.ds(CW * j, CW)
+            z[:, cols] = zbuf[ring, rows, cols] + rec_dot(prev, (0, 1), j)
+        if s == 0:
+            @pl.when(b + 1 < NBLK)
+            def _():
+                wait_block(layer, nxt)
+        in_product(nxt, 1 - ring, SHARE[s])
+        if layer == 0:
+            seq_step(b, s)
+
+        def add(*ks):
+            for j in range(NCHUNK):
+                z[:, pl.ds(CW * j, CW)] += rec_dot(prev, ks, j)
+
+        wait_for((NEXT_Y, 0))
+        add(4)
+        wait_for((NEXT_X, 0), (NEXT_Y, 1))
+        add(2, 5)
+        wait_for((DIAG, 0), (NEXT_Y, 2), (NEXT_X, 1), (NEXT_X, 2), (DIAG, 1), (DIAG, 2))
         new, part = [], []
 
         def products(*chunks):
             for j in chunks:
-                part.append(rec_dot(prev, (6, 3, 7, 8, 9), j))
+                part.append(rec_dot(prev, (3, 6, 7, 8, 9), j))
 
         def cell(j):
             units = pl.ds(LANES * j, LANES)
@@ -312,6 +357,15 @@
         send_h(s, 1)
         cell(4)
         send_h(s, 2)
+        if layer == 0:
+            if s == 0:
+                @pl.when(b > 0)
+                def _():
+                    for cp in pass_on(jnp.maximum(b - 1, 0), TB - 1, prev):
+                        cp.start()
+            else:
+                for cp in pass_on(b, s - 1, prev):
+                    cp.start()
         if layer == 1:
             near, far = split_units(lambda n: new[n])
             for n in range(3):
@@ -321,13 +375,21 @@
                 for cp in out_copies(b, ring):
                     cp.start()
 
-    def run_layer(layer):
+    def take_all(buf, layer, mat):
+        for cross in range(2):
+            for src_core in (1, 0):
+                take_weights(buf, layer == 1 or mat == 1, mat, cross, src_core)
+
+    def first_input():
         for ks in SHARE:
             in_product(0, 0, ks)
 
+    def run_layer(layer):
         def block(b, carry):
             if layer == 0:
-                @pl.when((b > 0) & (b + LEAD - 1 < NBLK))
+                last = jnp.where(crosses_here(b + LEAD), NBLK - LEAD, NBLK - LEAD + 1)
+
+                @pl.when((b > 0) & (b < last))
                 def _():
                     for s in range(TB):
                         seq_sent(s, s)
@@ -336,6 +398,8 @@
             return carry
 
         lax.fori_loop(0, NBLK, block, 0)
+
+    def leave_exchange(layer):
         slot = TB - 1
         for peer in range(3):
             for part in range(3):
@@ -358,8 +422,9 @@
         for i in range(2):
             for n in range(3):
                 hcraw[0, i, :, pl.ds(LANES * n, LANES)] = parts[i][n]
-        kept = pltpu.make_async_copy(hcraw.at[0, keep], out, c_send.at[0])
-        given = remote(hcraw.at[0, give], out, c_send.at[1], c_recv, PARTNER)
+        wide = pl.ds(0, PAD)
+        kept = pltpu.make_async_copy(hcraw.at[0, keep, :, wide], out, c_send.at[0])
+        given = remote(hcraw.at[0, give, :, wide], out, c_send.at[1], c_recv, PARTNER)
         kept.start()
         given.start()
         kept.wait()
@@ -380,16 +445,21 @@
     @pl.when(core == 0)
     def _():
         local = seq_copies(0, 0, None, None)
-        local.append(pltpu.make_async_copy(bias.at[0], braw.at[0], small_recv.at[0, 0]))
-        local.append(pltpu.make_async_copy(hc.at[0], hcraw.at[0], small_recv.at[1, 0]))
+        local += small_copies(0, 0, None)
         local += w_copies(0, False, 0, w_in1, 0, own_cols, win, None, 0)
         local += w_copies(1, True, 0, w_rec1, 0, own_cols, wrec, None, 0)
-        sent = [
-            remote(bias.at[1], braw.at[0], small_send.at[0], small_recv.at[0, 0], PARTNER),
-            remote(hc.at[1], hcraw.at[0], small_send.at[1], small_recv.at[1, 0], PARTNER),
-            remote(w_in2.at[:, far_cols], stage.at[0], st_send.at[0], st_recv.at[0], PARTNER),
-            remote(w_rec2.at[:, far_cols], stage.at[1], st_send.at[1], st_recv.at[1], PARTNER),
-        ]
+        sent = small_copies(1, 0, PARTNER)
+        more = []
+        for mat, ref, buf in ((0, w_in2, win), (1, w_rec2, wrec)):
+            for half in range(2):
+                rows = pl.ds(half * UNIT, UNIT)
+                if (mat, half) in DIRECT:
+                    dst = buf.at[pl.ds(place(True, 1, 0, half, 0), UNIT), :]
+                    recv = w_recv.at[mat, 1, 0, half, 0]
+                    more.append(remote(ref.at[rows, far_cols], dst, st_send.at[mat, half], recv, OVER))
+                else:
+                    dst, recv = stage.at[mat, rows, :], st_recv.at[mat, half]
+                    sent.append(remote(ref.at[rows, far_cols], dst, st_send.at[mat, half], recv, PARTNER))
         sent += w_copies(0, True, 0, w_in2, 0, own_cols, win, PARTNER, 4)
         sent += w_copies(1, True, 0, w_rec2, 0, own_cols, wrec, PARTNER, 6)
         cross_in = w_copies(0, False, 0, w_in1, 1, far_cols, win, ACROSS, 0)
@@ -399,38 +469,51 @@
         for rel in range(2):
             for i in range(3):
                 arrived(a8.at[:, 2 * rel + i] if i < 2 else a4.at[:, rel], seq_recv.at[rel, i])
-        for b in range(LEAD):
+        for n in range(2):
             for i in range(TB):
-                for cp in seq_pieces(b, i, TB + TB * b + i):
+                for cp in seq_pieces(col + 2 * n, i, TB * (n + 1) + i, False):
                     cp.start()
         for cp in cross_rec:
             cp.start()
         begin()
-        for mat, buf in enumerate((win, wrec)):
-            for cross in range(2):
-                for src_core in range(2):
-                    take_weights(buf, mat == 1, mat, cross, src_core)
+        for cp in more:
+            cp.start()
+
+        def hand_on(n):
+            block_arrived(0, col + 2 * n)
+            for i in range(TB):
+                for cp in seq_pieces(col + 2 * n, i, TB * (n + 3) + i, True):
+                    cp.start()
+
+        hand_on(0)
+        pl.when(col == 0)(lambda: hand_on(1))
+        take_all(win, 0, 0)
         wait_block(0, 0)
+        first_input()
+        take_all(wrec, 0, 1)
         run_layer(0)
+        leave_exchange(0)
         end(0, 1, c1_out, c2_out)
         arrived(h2_out, o_recv)
-        for b in range(LEAD):
+        for n in range(3):
             for i in range(TB):
-                seq_sent(i, TB + TB * b + i)
-        for cp in sent + cross_in + cross_rec:
+                seq_sent(i, TB * (n + 1) + i)
+
+        @pl.when(col == 0)
+        def _():
+            for i in range(TB):
+                seq_sent(i, 4 * TB + i)
+
+        for cp in sent + cross_in + cross_rec + more:
             cp.wait_send()
 
     @pl.when(core == 1)
     def _():
-        local = [
-            pltpu.make_async_copy(bias.at[1], braw.at[1], small_recv.at[0, 1]),
-            pltpu.make_async_copy(hc.at[1], hcraw.at[1], small_recv.at[1, 1]),
-        ]
+        local = small_copies(1, 1, None)
         local += w_copies(0, True, 1, w_in2, 0, own_cols, win, None, 0)
         local += w_copies(1, True, 1, w_rec2, 0, own_cols, wrec, None, 0)
-        sent = seq_copies(0, 1, PARTNER, [small_send.at[2 + i] for i in range(3)])
-        sent.append(remote(bias.at[0], braw.at[1], small_send.at[0], small_recv.at[0, 1], PARTNER))
-        sent.append(remote(hc.at[0], hcraw.at[1], small_send.at[1], small_recv.at[1, 1], PARTNER))
+        sent = seq_copies(0, 1, PARTNER, [small_send.at[3 + i] for i in range(3)])
+        sent += small_copies(0, 1, PARTNER)
         sent += w_copies(0, False, 1, w_in1, 1, far_cols, win, OVER, 0)
         sent += w_copies(1, True, 1, w_rec1, 1, far_cols, wrec, OVER, 2)
         sent += w_copies(0, False, 1, w_in1, 0, own_cols, win, PARTNER, 4)
@@ -440,26 +523,33 @@
             cp.start()
         late = w_copies(0, True, 1, w_in2, 1, far_cols, win, ACROSS, 8)
         for mat, buf, more in ((0, win, late_rec), (1, wrec, [])):
-            arrived(stage.at[mat], st_recv.at[mat])
             for half in range(2):
-                rows = pl.ds(place(True, 1, 0, half, 0), UNIT)
-                src = stage.at[mat, pl.ds(half * UNIT, UNIT), :]
-                late.append(remote(src, buf.at[rows, :], fw_send.at[mat, half], w_recv.at[mat, 1, 0, half, 0], ACROSS))
+                if (mat, half) not in DIRECT:
+                    rows = pl.ds(place(True, 1, 0, half, 0), UNIT)
+                    src = stage.at[mat, pl.ds(half * UNIT, UNIT), :]
+                    arrived(src, st_recv.at[mat, half])
+                    recv = w_recv.at[mat, 1, 0, half, 0]
+                    late.append(remote(src, buf.at[rows, :], fw_send.at[mat, half], recv, ACROSS))
             late += more
         for cp in late:
             cp.start()
         begin()
-        for mat, buf in enumerate((win, wrec)):
-            for cross in range(2):
-                for src_core in (1, 0):
-                    take_weights(buf, True, mat, cross, src_core)
+        take_all(win, 1, 0)
         wait_block(1, 0)
+        first_input()
+        take_all(wrec, 1, 1)
         run_layer(1)
+        end(1, 0, c2_out, c1_out)
         for b in (NBLK - 2, NBLK - 1):
             out_wait(b, b % 2)
-        end(1, 0, c2_out, c1_out)
+        leave_exchange(1)
         for cp in sent + late:
             cp.wait_send()
+
+
+def _trim(c1_in, c2_in, c1_out, c2_out):
+    c1_out[...] = c1_in[:, :UNIT]
+    c2_out[...] = c2_in[:, :UNIT]
 
 
 def solution(mesh):
@@ -468,11 +558,6 @@
     vmem = pltpu.VMEM
 
     def local_program(seq_in, w_in1, w_rec1, b_gate1, w_in2, w_rec2, b_gate2, h_init, c_init):
-        col = lax.axis_index("col")
-        states = jnp.stack([h_init, c_init], axis=1)
-        states = lax.dynamic_slice_in_dim(states, col * UNIT, UNIT, axis=3)
-        states = jnp.pad(states, ((0, 0), (0, 0), (0, 0), (0, PAD - UNIT)))
-        bias = jnp.broadcast_to(jnp.stack([b_gate1, b_gate2])[:, None, :], (2, 8, 4 * UNIT))
         seq = seq_in.reshape(NBLK, ROWS, CHIP)
         h2, c1, c2, _ = pl.pallas_call(
             _kernel,
@@ -482,7 +567,7 @@
                 jax.ShapeDtypeStruct((BATCH, PAD), F32),
                 jax.ShapeDtypeStruct((2, CHIP, GATES), BF16),
             ),
-            in_specs=[any_spec] * 7,
+            in_specs=[any_spec] * 9,
             out_specs=(any_spec,) * 4,
             scratch_shapes=[
                 vmem((HIDDEN, GATES), BF16),
@@ -495,20 +580,20 @@
                 vmem((TB, 4, BATCH, LANES), BF16),
                 vmem((BATCH, CHIP), F32),
                 vmem((8, GATES), F32),
-                vmem((2, 8, 4 * UNIT), F32),
-                vmem((2, 2, BATCH, PAD), F32),
+                vmem((2, 4 * UNIT // LANES, LANES), F32),
+                vmem((2, 2, BATCH, CHIP), F32),
                 vmem((2, ROWS, PAD), BF16),
                 vmem((2, ROWS, PAD), BF16),
                 vmem((TB * HIDDEN // 8, LANES), F32),
                 dma((2, 2, 2, 2, 2)),
                 dma((12, 2)),
-                dma((2,)),
-                dma((2,)),
                 dma((2, 2)),
                 dma((2, 2)),
-                dma((5,)),
+                dma((2, 2)),
                 dma((2, 3)),
-                dma((TB + TB * LEAD,)),
+                dma((6,)),
+                dma((2, 3)),
+                dma((5 * TB,)),
                 dma((NBLK,)),
                 dma((TB, 3, 3)),
                 dma((TB,)),
@@ -521,8 +606,10 @@
             compiler_params=pltpu.CompilerParams(
                 collective_id=0, has_side_effects=True, vmem_limit_bytes=62 * 2**20
             ),
-        )(seq, w_in1, w_rec1, w_in2, w_rec2, bias, states)
-        return h2.reshape(STEPS, BATCH, PAD)[:, :, :UNIT], c1[:, :UNIT], c2[:, :UNIT]
+        )(seq, w_in1, w_rec1, w_in2, w_rec2, b_gate1.reshape(-1, LANES), b_gate2.reshape(-1, LANES), h_init, c_init)
+        cell = jax.ShapeDtypeStruct((BATCH, UNIT), F32)
+        c1, c2 = pl.pallas_call(_trim, out_shape=(cell, cell))(c1, c2)
+        return h2.reshape(STEPS, BATCH, PAD)[:, :, :UNIT], c1, c2
 
     row_spec = P(None, "dp", "row")
     weight_spec = P("row", "col")

time: 888 us -> 842 us (0.948)
  Pallas kernels: 876 us -> 836 us
    pallas_call x1, Pallas kernels: 876 us -> 835 us  [local_program(): pl.pallas_call(_kernel, out_shape=(jax.ShapeDtypeStruct((NBLK, ROWS, PAD)...]
where the time goes in v2:
time: 842 us
  Pallas kernels  836 us (99%)
    pallas_call x1, Pallas kernels, local_program(): pl.pallas_call(_kernel, out_shape=(jax.ShapeDtypeStruct((NBLK, ROWS, PAD)...  835 us

profile of v2, /device:TPU:0, one launch (start us, length us, event | category | flops | bytes accessed | tf_op | source)
XLA Modules:
  0.0 841.8 jit_solution(18156767847096911488)
XLA Ops:
  0.6 834.9 %shard_map.112 = (bf16[32,128,384]{2,1,0:T(8,128)(2,1)}, f32[32,384]{1,0:T(8,128)}, f32[32,384]{1,0:T(8,128)}, bf16[2,640,2560]{2,1,0:T(8,128)(2,1)}) custom-call(bf16[32,128,640]{2,1,0:T(8,128)(2,1)} %bitcast.5, bf16[640,5120]{1,0:T(8,128)(2,1)} %w_in1.1, bf16[640,5120]{1,0:T(8,128)(2,1)} %w_rec1.1, bf16[640,5120]{1,0:T(8,128)(2,1)} %w_in2.1, ...), custom_call_target="tpu_custom_call" | custom-call | tf_op jit(solution)/shard_map/pallas_call | solution.py:562
  835.5 4.8 copy.13
  840.3 1.5 shard_map.113

commit v3 on v2

--- a/solution.py
+++ b/solution.py
@@ -9,6 +9,7 @@
 F32, BF16 = jnp.float32, jnp.bfloat16
 LANES = 128
 TILE = 256
+NTILE = 10
 STEPS, BATCH, HIDDEN = 128, 32, 2560
 UNIT = 320
 CHIP = 2 * UNIT
@@ -17,12 +18,16 @@
 NBLK = STEPS // TB
 ROWS = TB * BATCH
 LEAD = 3
-DIRECT = ((0, 0),)
+DIRECT = ((0, 0), (0, 1))
 NCHUNK = CHIP // LANES
 MAIN = 2 * TILE
 REST = CHIP - MAIN
 CW = 4 * LANES
 SHARE = ((0, 1, 2), (3, 4, 5), (6, 7), (8, 9))
+HALVES = (range(5), range(5, NTILE))
+PAIR = 2 * BATCH
+BOTH = range(2)
+SQUARE = (2, 2)
 PAD = 3 * LANES
 FILL = 96
 PARTNER, ACROSS, OVER, ALONG = (0, 1, 0), (1, 0, 0), (1, 1, 0), (0, 0, 1)
@@ -83,7 +88,7 @@
         arrived(size.at[pl.ds(0, units // 8)], sem)
 
     barrier = pltpu.get_barrier_semaphore()
-    others = [(dx, dc, dy) for dx in range(2) for dc in range(2) for dy in range(2) if dx + dc + dy]
+    others = [(dx, dc, dy) for dx in BOTH for dc in BOTH for dy in BOTH if dx + dc + dy]
     for to in others:
         pl.semaphore_signal(barrier, inc=1, device_id=device(*to), device_id_type=MESH)
     pl.semaphore_wait(barrier, len(others))
@@ -107,7 +112,7 @@
 
     def w_copies(mat, by_unit, src_core, ref, cross, cols, buf, to, send_base):
         out = []
-        for half in range(2):
+        for half in BOTH:
             for i, (start, rows, unit) in enumerate(pieces(by_unit, src_core, half)):
                 src = ref.at[pl.ds(start, rows), cols]
                 dst = buf.at[pl.ds(place(by_unit, cross, src_core, half, unit), rows), :]
@@ -119,7 +124,7 @@
         return out
 
     def take_weights(buf, by_unit, mat, cross, src_core):
-        for half in range(2):
+        for half in BOTH:
             for i, (_, count, unit) in enumerate(pieces(by_unit, src_core, half)):
                 off = place(by_unit, cross, src_core, half, unit)
                 arrived(buf.at[pl.ds(off, count), :], w_recv.at[mat, cross, src_core, half, i])
@@ -150,14 +155,21 @@
         rows = jnp.concatenate([tiles_of(h8, h4, slot, ks), jnp.zeros((FILL, TILE * len(ks)), BF16)], axis=0)
         return jnp.dot(rows, rows_of(wrec, ks, j), preferred_element_type=F32)[:BATCH]
 
-    def in_product(block, into, ks):
+    def in_product(block, into, ks, half=None):
+        used = ROWS if half is None else PAIR
         for j in range(NCHUNK):
             cols = pl.ds(CW * j, CW)
-            part = jnp.dot(tiles_of(a8, a4, block, ks), rows_of(win, ks, j), preferred_element_type=F32)
+            if half is None:
+                rows = tiles_of(a8, a4, block, ks)
+            else:
+                part_of = pl.ds(PAIR * half, PAIR)
+                rows = tiles_of(a8.at[:, :, part_of], a4.at[:, :, part_of], block, ks)
+                rows = jnp.concatenate([rows, jnp.zeros_like(rows)], axis=0)
+            part = jnp.dot(rows, rows_of(win, ks, j), preferred_element_type=F32)[:used]
             if ks[0] == 0:
-                zbuf[into, :, cols] = part + bias_s[0:1, cols]
+                zbuf[into, pl.ds(0, used), cols] = part + bias_s[0:1, cols]
             else:
-                zbuf[into, :, cols] += part
+                zbuf[into, pl.ds(0, used), cols] += part
 
     def put_h(slot, chunk, v):
         if chunk < 4:
@@ -166,7 +178,7 @@
             h4[slot, 0] = v.astype(BF16)
 
     def small_setup():
-        for src_core in range(2):
+        for src_core in BOTH:
             for i, ref in enumerate((braw.at[src_core], hcraw.at[src_core, 0], hcraw.at[src_core, 1])):
                 arrived(ref, small_recv.at[src_core, i])
 
@@ -177,7 +189,7 @@
             bias_s[:, pl.ds(LANES * n, LANES)] = v
 
         _repack(get_bias, put_bias)
-        for which in range(2):
+        for which in BOTH:
             def get(n):
                 return hcraw[n // NCHUNK, which, :, pl.ds(LANES * (n % NCHUNK), LANES)]
 
@@ -233,8 +245,8 @@
     def pass_on(block, s, slot):
         rows = pl.ds(BATCH * s, BATCH)
         return (
-            remote(h8.at[slot], a8.at[block, :, rows, :], d_send.at[slot], a_recv.at[block], PARTNER),
-            remote(h4.at[slot], a4.at[block, :, rows, :], d_send.at[slot], a_recv.at[block], PARTNER),
+            remote(h8.at[slot], a8.at[block, :, rows, :], d_send.at[slot], a_recv.at[2 * block + s // 2], PARTNER),
+            remote(h4.at[slot], a4.at[block, :, rows, :], d_send.at[slot], a_recv.at[2 * block + s // 2], PARTNER),
         )
 
     def passed_on(slot):
@@ -263,21 +275,21 @@
         def _():
             block = jnp.minimum(behind, NBLK - 1)
             if s == 0:
-                block_arrived(0, block)
+                block_arrived(block)
             for cp in seq_pieces(block, s, s, True):
                 cp.start()
 
     def seq_sent(i, send):
         units_moved(TB * (TILE + LANES if i < 2 else TILE), seq_send.at[send])
 
-    def block_arrived(layer, block):
-        units_moved(TB * (HIDDEN if layer else HIDDEN // 2), a_recv.at[block])
-
-    def wait_block(layer, block):
-        if layer == 0:
-            pl.when(jnp.logical_not(crosses_here(block)))(lambda: block_arrived(layer, block))
-        else:
-            block_arrived(layer, block)
+    def block_arrived(block):
+        units_moved(TB * HIDDEN // 2, a_recv.at[block])
+
+    def wait_block(block):
+        pl.when(jnp.logical_not(crosses_here(block)))(lambda: block_arrived(block))
+
+    def pair_arrived(block, half):
+        units_moved(2 * HIDDEN, a_recv.at[2 * block + half])
 
     def out_copies(block, ring):
         return (
@@ -311,14 +323,22 @@
                 pl.when(b > 0)(lambda: passed_on((s + 1) % TB))
         if layer == 1 and s == 0:
             pl.when(b > 1)(lambda: out_wait(jnp.maximum(b - 2, 0), ring))
+        pair, odd = divmod(s, 2)
+        from_z = zbuf.at[pair, pl.ds(BATCH * odd, BATCH)] if layer else zbuf.at[ring, rows]
         for j in range(NCHUNK):
             cols = pl.ds(CW * j, CW)
-            z[:, cols] = zbuf[ring, rows, cols] + rec_dot(prev, (0, 1), j)
-        if s == 0:
-            @pl.when(b + 1 < NBLK)
-            def _():
-                wait_block(layer, nxt)
-        in_product(nxt, 1 - ring, SHARE[s])
+            z[:, cols] = from_z[:, cols] + rec_dot(prev, (0, 1), j)
+        if layer:
+            target = nxt if pair else b
+            if s == 0:
+                pair_arrived(b, 1)
+            elif s == 2:
+                pl.when(b + 1 < NBLK)(lambda: pair_arrived(nxt, 0))
+            in_product(target, 1 - pair, HALVES[odd], 1 - pair)
+        else:
+            if s == 0:
+                pl.when(b + 1 < NBLK)(lambda: wait_block(nxt))
+            in_product(nxt, 1 - ring, SHARE[s])
         if layer == 0:
             seq_step(b, s)
 
@@ -376,13 +396,9 @@
                     cp.start()
 
     def take_all(buf, layer, mat):
-        for cross in range(2):
+        for cross in BOTH:
             for src_core in (1, 0):
                 take_weights(buf, layer == 1 or mat == 1, mat, cross, src_core)
-
-    def first_input():
-        for ks in SHARE:
-            in_product(0, 0, ks)
 
     def run_layer(layer):
         def block(b, carry):
@@ -419,7 +435,7 @@
 
     def end(keep, give, out, other):
         parts = split_units(lambda n: c_s[:, pl.ds(LANES * n, LANES)])
-        for i in range(2):
+        for i in BOTH:
             for n in range(3):
                 hcraw[0, i, :, pl.ds(LANES * n, LANES)] = parts[i][n]
         wide = pl.ds(0, PAD)
@@ -451,7 +467,7 @@
         sent = small_copies(1, 0, PARTNER)
         more = []
         for mat, ref, buf in ((0, w_in2, win), (1, w_rec2, wrec)):
-            for half in range(2):
+            for half in BOTH:
                 rows = pl.ds(half * UNIT, UNIT)
                 if (mat, half) in DIRECT:
                     dst = buf.at[pl.ds(place(True, 1, 0, half, 0), UNIT), :]
@@ -466,10 +482,10 @@
         cross_rec = w_copies(1, True, 0, w_rec1, 1, far_cols, wrec, ACROSS, 2)
         for cp in cross_in + local + sent:
             cp.start()
-        for rel in range(2):
+        for rel in BOTH:
             for i in range(3):
                 arrived(a8.at[:, 2 * rel + i] if i < 2 else a4.at[:, rel], seq_recv.at[rel, i])
-        for n in range(2):
+        for n in BOTH:
             for i in range(TB):
                 for cp in seq_pieces(col + 2 * n, i, TB * (n + 1) + i, False):
                     cp.start()
@@ -480,7 +496,7 @@
             cp.start()
 
         def hand_on(n):
-            block_arrived(0, col + 2 * n)
+            block_arrived(col + 2 * n)
             for i in range(TB):
                 for cp in seq_pieces(col + 2 * n, i, TB * (n + 3) + i, True):
                     cp.start()
@@ -488,8 +504,9 @@
         hand_on(0)
         pl.when(col == 0)(lambda: hand_on(1))
         take_all(win, 0, 0)
-        wait_block(0, 0)
-        first_input()
+        wait_block(0)
+        for ks in SHARE:
+            in_product(0, 0, ks)
         take_all(wrec, 0, 1)
         run_layer(0)
         leave_exchange(0)
@@ -523,7 +540,7 @@
             cp.start()
         late = w_copies(0, True, 1, w_in2, 1, far_cols, win, ACROSS, 8)
         for mat, buf, more in ((0, win, late_rec), (1, wrec, [])):
-            for half in range(2):
+            for half in BOTH:
                 if (mat, half) not in DIRECT:
                     rows = pl.ds(place(True, 1, 0, half, 0), UNIT)
                     src = stage.at[mat, pl.ds(half * UNIT, UNIT), :]
@@ -535,8 +552,9 @@
             cp.start()
         begin()
         take_all(win, 1, 0)
-        wait_block(1, 0)
-        first_input()
+        pair_arrived(0, 0)
+        for ks in HALVES:
+            in_product(0, 0, ks, 0)
         take_all(wrec, 1, 1)
         run_layer(1)
         end(1, 0, c2_out, c1_out)
@@ -587,19 +605,17 @@
                 vmem((TB * HIDDEN // 8, LANES), F32),
                 dma((2, 2, 2, 2, 2)),
                 dma((12, 2)),
-                dma((2, 2)),
-                dma((2, 2)),
-                dma((2, 2)),
+                *[dma(SQUARE)] * 3,
                 dma((2, 3)),
                 dma((6,)),
                 dma((2, 3)),
                 dma((5 * TB,)),
-                dma((NBLK,)),
+                dma((2 * NBLK,)),
                 dma((TB, 3, 3)),
                 dma((TB,)),
                 dma((TB,)),
                 dma(()),
-                dma((2, 2)),
+                dma(SQUARE),
                 dma(()),
                 dma((2,)),
             ],

time: 842 us -> 840 us (level)
  no operation moved by 1% of the time
where the time goes in v3:
time: 840 us; the launch traced here: 839 us
  Pallas kernels  834 us (99%)
    pallas_call x1, Pallas kernels, local_program(): pl.pallas_call(_kernel, out_shape=(jax.ShapeDtypeStruct((NBLK, ROWS, PAD)...  832 us

profile of v3, /device:TPU:0, one launch (start us, length us, event | category | flops | bytes accessed | tf_op | source)
XLA Modules:
  0.0 839.1 jit_solution(5955477588017759454)
XLA Ops:
  0.6 832.2 %shard_map.112 = (bf16[32,128,384]{2,1,0:T(8,128)(2,1)}, f32[32,384]{1,0:T(8,128)}, f32[32,384]{1,0:T(8,128)}, bf16[2,640,2560]{2,1,0:T(8,128)(2,1)}) custom-call(bf16[32,128,640]{2,1,0:T(8,128)(2,1)} %bitcast.5, bf16[640,5120]{1,0:T(8,128)(2,1)} %w_in1.1, bf16[640,5120]{1,0:T(8,128)(2,1)} %w_rec1.1, bf16[640,5120]{1,0:T(8,128)(2,1)} %w_in2.1, ...), custom_call_target="tpu_custom_call" | custom-call | tf_op jit(solution)/shard_map/pallas_call | solution.py:580
  832.8 4.8 copy.13
  837.6 1.5 shard_map.113
